TPU v7x, 128 devices: a whole 4x4x4 slice. The times are simulated.
128 devices in a mesh: row: 8 (over y_hi, z), col: 16 (over y_lo, x, core).
Axes of the slice: x: 4, y: 4 (y_hi: 2, y_lo: 2; y = y_hi * 2 + y_lo), z: 4, core: 2. Of those that a mesh axis runs over, the one named last changes fastest.
Arguments:
- build_key: int32 [16, 16, 128], P('col', 'row'), may hold values from -1 to 63, as said below
- build_part: int32 [16, 16], P('col', 'row'), may hold values from 0 to 1023, as said below
- build_payload: float32 [16, 16, 128, 128], P('col', 'row'), may hold values from -6 to 6
- probe_key: int32 [8, 16, 16, 8, 128], P('row', 'col'), may hold values from -2 to 63, as said below
- probe_part: int32 [8, 16, 16, 8, 128], P('row', 'col'), may hold values from 0 to 1023, as said below
Outputs:
- joined: float32 [8, 16, 16, 8, 128, 128], P('row', 'col')
- match_position: float32 [8, 16, 16, 8, 128], P('row', 'col')
- match_rate: float32 [1024], replicated
Inputs may be any that keep to these rules, and one draw needn't show every extreme that they name: Each column c owns a set of 64 partitions, disjoint from the other columns' sets; build_part[c, t] lies in column c's set. `build_key`: -1 marks padding rows, which lie at the end of a tile. `probe_key`: -2 marks padding rows, which lie at the end of a tile. probe_part[r, s, c, q, i] lies in the set of partitions owned by column c.
All inputs are finite; a program needn't handle non-finite values.
Results may differ from a plain program's by a relative error of at most 0.0003.
Values sent between devices are 32-bit elements; how exact they have to be, the bound alone decides.
A program may use at most 256 MiB of HBM per device.

v0:
```python
import math

import jax
import jax.numpy as jnp
from jax import lax
from jax.sharding import Mesh
from jax.sharding import PartitionSpec as P

PARTS_SIZE = 1024
ROW = ("row_0", "row_1")
COL = ("col_0", "col_1", "col_2")
ROW_COL = ("row_0", "row_1", "col_0", "col_1", "col_2")


def in_one_piece(arrays, axis, split_dim, concat_dim, along):
    widths = [a.shape[along] for a in arrays]
    both = jnp.concatenate(arrays, axis=along)
    whole = lax.all_to_all(both, axis, split_axis=split_dim, concat_axis=concat_dim, tiled=True)
    return tuple(jnp.split(whole, [sum(widths[:k]) for k in range(1, len(widths))], axis=along))


def in_one_piece_2(arrays, axis, dim, along):
    widths = [math.prod(a.shape[along:]) for a in arrays]
    both = jnp.concatenate(
        [a.reshape(*a.shape[:along], w) for a, w in zip(arrays, widths)], axis=along
    )
    whole = lax.all_gather(both, axis, axis=dim, tiled=True)
    blocks = jnp.split(whole, [sum(widths[:k]) for k in range(1, len(widths))], axis=along)
    return tuple(
        (b.reshape(*whole.shape[:along], *a.shape[along:]) for a, b in zip(arrays, blocks))
    )


def sent_together(arrays, axis, split_dim, concat_dim, along):
    widths = [math.prod(a.shape[along:]) for a in arrays]
    both = jnp.concatenate(
        [a.reshape(*a.shape[:along], w) for a, w in zip(arrays, widths)], axis=along
    )
    whole = lax.all_to_all(both, axis, split_axis=split_dim, concat_axis=concat_dim, tiled=True)
    blocks = jnp.split(whole, [sum(widths[:k]) for k in range(1, len(widths))], axis=along)
    return tuple(
        (b.reshape(*whole.shape[:along], *a.shape[along:]) for a, b in zip(arrays, blocks))
    )


def over_axes(array, axes):
    for axis in axes:
        array = lax.psum(array, axis)
    return array


def tile_join(probe_keys, probe_parts, build_keys, build_parts, payload, positions):
    count_tiles = build_keys.shape[0]
    tile_rows = build_keys.shape[1]
    flat_keys = build_keys.reshape(-1)
    flat_parts = jnp.broadcast_to(build_parts.reshape(-1, 1), (count_tiles, tile_rows)).reshape(-1)
    flat_payload = payload.reshape(count_tiles * tile_rows, payload.shape[-1])
    side_columns = jnp.stack([positions, jnp.ones_like(positions)], axis=1)

    def tile_one_block(block_args):
        block_keys, block_parts = block_args
        matched = (
            (block_keys[:, None] == flat_keys[None, :])
            & (block_parts[:, None] == flat_parts[None, :])
        ).astype(jnp.float32)
        summed = jnp.dot(
            matched,
            flat_payload,
            precision=lax.Precision.HIGHEST,
            preferred_element_type=jnp.float32,
        )
        sidebar = jnp.dot(
            matched,
            side_columns,
            precision=lax.Precision.HIGHEST,
            preferred_element_type=jnp.float32,
        )
        return (summed, sidebar[:, 0], sidebar[:, 1])

    return lax.map(tile_one_block, (probe_keys, probe_parts))


def place_rows(tile_count, tile_rows, whole_rows):
    offsets = jnp.arange(tile_count * tile_rows, dtype=jnp.int32)
    return offsets.astype(jnp.float32) / float(whole_rows)


def add_pieces(probe_keys, probe_parts, pieces, positions):
    piece_keys, piece_parts, piece_payload = pieces
    summed, placed, counted = tile_join(
        probe_keys, probe_parts, piece_keys[0], piece_parts[0], piece_payload[0], positions
    )
    return (summed, placed, counted)


def partition_sums(part_ids, values, blocks):
    block_ids = part_ids.reshape(blocks, -1)
    block_values = values.reshape(blocks, block_ids.shape[1], values.shape[-1])
    labels = jnp.arange(PARTS_SIZE, dtype=jnp.int32)

    def partition_one_block(block_args):
        ids_here, values_here = block_args
        onehot = (labels[:, None] == ids_here[None, :]).astype(jnp.float32)
        return jnp.dot(
            onehot, values_here, precision=lax.Precision.HIGHEST, preferred_element_type=jnp.float32
        )

    return jnp.sum(lax.map(partition_one_block, (block_ids, block_values)), axis=0)


def local(build_key, build_part, build_payload, probe_key, probe_part):
    build_keys = build_key.astype(jnp.float32)
    build_parts = build_part.astype(jnp.float32)
    columns = build_payload.shape[-1]
    tile_rows = build_key.shape[-1]
    local_tiles = build_key.shape[1]
    whole_rows = local_tiles * lax.axis_size(ROW) * tile_rows
    owners = probe_key.shape[2]
    probe_tiles = probe_key.shape[3]
    got_keys, got_parts = in_one_piece((probe_key, probe_part), COL, 2, 1, 0)
    probe_keys = got_keys.reshape(owners, probe_tiles * tile_rows).astype(jnp.float32)
    probe_parts = got_parts.reshape(owners, probe_tiles * tile_rows).astype(jnp.float32)
    pieces = in_one_piece_2((build_keys, build_parts, build_payload), ROW, 1, 2)
    positions = place_rows(pieces[0].shape[1], tile_rows, whole_rows)
    summed, placed, counted = add_pieces(probe_keys, probe_parts, pieces, positions)
    joined = summed.reshape(1, owners, 1, probe_tiles, tile_rows, columns)
    places = placed.reshape(1, owners, 1, probe_tiles, tile_rows)
    counts = counted.reshape(1, owners, 1, probe_tiles, tile_rows)
    back_joined, back_places, back_counts = sent_together((joined, places, counts), COL, 1, 2, 5)
    part_ids = probe_part.reshape(-1)
    live_rows = (probe_key >= 0).astype(jnp.float32).reshape(-1)
    both_columns = jnp.stack([back_counts.reshape(-1), live_rows], axis=1)
    local_sums = partition_sums(part_ids, both_columns, owners)
    match_total, live_total = (
        over_axes(local_sums[:, 0], ROW_COL),
        over_axes(local_sums[:, 1], ROW_COL),
    )
    return (back_joined, back_places, match_total / jnp.maximum(live_total, 1.0))


def solution(mesh):
    finer = Mesh(mesh.devices.reshape(2, 4, 2, 4, 2), ("row_0", "row_1", "col_0", "col_1", "col_2"))
    return jax.shard_map(
        local,
        mesh=finer,
        in_specs=(
            P(COL, ROW, None),
            P(COL, ROW),
            P(COL, ROW, None, None),
            P(ROW, COL, None, None, None),
            P(ROW, COL, None, None, None),
        ),
        out_specs=(P(ROW, COL, None, None, None, None), P(ROW, COL, None, None, None), P()),
        check_vma=False,
    )
```

profile of v0, /device:TPU:1, one launch (start us, length us, event | category | flops | bytes accessed | tf_op | source)
XLA Modules:
  0.0 442.2 jit_solution(15169390662300997856)
XLA Ops:
  12.2 6.8 %all-to-all-start = ((s32[2,1,16,8,128]{4,3,1,0,2:T(8,128)}), s32[2,1,16,8,128]{4,3,1,0,2:T(8,128)S(1)}, u32[]{:S(2)}, u32[]{:S(2)}) async-start(s32[2,1,16,8,128]{4,3,1,0,2:T(8,128)} %pad_add_fusion), calls=%async_computation | async-start | bytes 262144 | tf_op jit(solution)/shard_map/all_to_all | solution.py:18
  19.1 6.0 %all-to-all-done = s32[2,1,16,8,128]{4,3,1,0,2:T(8,128)S(1)} async-done(((s32[2,1,16,8,128]{4,3,1,0,2:T(8,128)}), s32[2,1,16,8,128]{4,3,1,0,2:T(8,128)S(1)}, u32[]{:S(2)}, u32[]{:S(2)}) %all-to-all-start) | async-done | bytes 131104 | tf_op jit(solution)/shard_map/all_to_all | solution.py:18
  25.2 33.9 %all-gather.2.cloned.1.call-done = f32[1,16,16513]{2,0,1:T(1,128)} async-done(((f32[1,2,16513]{2,0,1:T(1,128)}), f32[1,16,16513]{2,0,1:T(1,128)}) %all-gather.2.cloned.1.call-update) | async-done | bytes 1056848 | tf_op jit(solution)/shard_map/all_gather | solution.py:27
  64.1 150.1 %while.26 = (s32[]{:T(128)}, f32[16,1024,128]{2,1,0:T(8,128)}, f32[16,1024]{1,0:T(8,128)S(1)}, f32[16,1024]{1,0:T(8,128)S(1)}, f32[16,1024]{1,0:T(8,128)S(1)}, /...) while((s32[]{:T(128)}, f32[16,1024,128]{2,1,0:T(8,128)}, ...), condition=%wide.region_1.2_spmd.clone, body=%wide.region_0.1_spmd.clone.sunk | while | flops 3284140032 | bytes 1704641 | solution.py:80
  68.6 4.9 %fusion.35 = f32[16,1024,128]{2,1,0:T(8,128)} fusion(f32[16,1024,128]{2,1,0:T(8,128)} %get-tuple-element.297, s32[]{:T(128)} %get-tuple-element.296, f32[2048,128]{1,0:T(8,128)S(1)} %get-tuple-element.315, f32[2048]{0:T(1024)S(1)} %broadcast_bitcast_fusion.2, f32[2048]{0:T(1024)S(1)} %bitcast.108, f32[1024]{0:T(1024)S(1)} %bitcast.99, ...), kind=kOutput, calls=%fused_computation.14.clone.1 | convolution fusion | flops 3227516928 | bytes 1597952 | tf_op jit(solution)/shard_map/while/body/eval_jaxpr/dot_general | solution.py:66
  87.3 4.9 %fusion.35 = f32[16,1024,128]{2,1,0:T(8,128)} fusion(f32[16,1024,128]{2,1,0:T(8,128)} %get-tuple-element.297, s32[]{:T(128)} %get-tuple-element.296, f32[2048,128]{1,0:T(8,128)S(1)} %get-tuple-element.315, f32[2048]{0:T(1024)S(1)} %broadcast_bitcast_fusion.2, f32[2048]{0:T(1024)S(1)} %bitcast.108, f32[1024]{0:T(1024)S(1)} %bitcast.99, ...), kind=kOutput, calls=%fused_computation.14.clone.1 | convolution fusion | flops 3227516928 | bytes 1597952 | tf_op jit(solution)/shard_map/while/body/eval_jaxpr/dot_general | solution.py:66
  96.7 4.9 %fusion.35 = f32[16,1024,128]{2,1,0:T(8,128)} fusion(f32[16,1024,128]{2,1,0:T(8,128)} %get-tuple-element.297, s32[]{:T(128)} %get-tuple-element.296, f32[2048,128]{1,0:T(8,128)S(1)} %get-tuple-element.315, f32[2048]{0:T(1024)S(1)} %broadcast_bitcast_fusion.2, f32[2048]{0:T(1024)S(1)} %bitcast.108, f32[1024]{0:T(1024)S(1)} %bitcast.99, ...), kind=kOutput, calls=%fused_computation.14.clone.1 | convolution fusion | flops 3227516928 | bytes 1597952 | tf_op jit(solution)/shard_map/while/body/eval_jaxpr/dot_general | solution.py:66
  106.1 4.9 %fusion.35 = f32[16,1024,128]{2,1,0:T(8,128)} fusion(f32[16,1024,128]{2,1,0:T(8,128)} %get-tuple-element.297, s32[]{:T(128)} %get-tuple-element.296, f32[2048,128]{1,0:T(8,128)S(1)} %get-tuple-element.315, f32[2048]{0:T(1024)S(1)} %broadcast_bitcast_fusion.2, f32[2048]{0:T(1024)S(1)} %bitcast.108, f32[1024]{0:T(1024)S(1)} %bitcast.99, ...), kind=kOutput, calls=%fused_computation.14.clone.1 | convolution fusion | flops 3227516928 | bytes 1597952 | tf_op jit(solution)/shard_map/while/body/eval_jaxpr/dot_general | solution.py:66
  115.5 4.9 %fusion.35 = f32[16,1024,128]{2,1,0:T(8,128)} fusion(f32[16,1024,128]{2,1,0:T(8,128)} %get-tuple-element.297, s32[]{:T(128)} %get-tuple-element.296, f32[2048,128]{1,0:T(8,128)S(1)} %get-tuple-element.315, f32[2048]{0:T(1024)S(1)} %broadcast_bitcast_fusion.2, f32[2048]{0:T(1024)S(1)} %bitcast.108, f32[1024]{0:T(1024)S(1)} %bitcast.99, ...), kind=kOutput, calls=%fused_computation.14.clone.1 | convolution fusion | flops 3227516928 | bytes 1597952 | tf_op jit(solution)/shard_map/while/body/eval_jaxpr/dot_general | solution.py:66
  124.9 4.9 %fusion.35 = f32[16,1024,128]{2,1,0:T(8,128)} fusion(f32[16,1024,128]{2,1,0:T(8,128)} %get-tuple-element.297, s32[]{:T(128)} %get-tuple-element.296, f32[2048,128]{1,0:T(8,128)S(1)} %get-tuple-element.315, f32[2048]{0:T(1024)S(1)} %broadcast_bitcast_fusion.2, f32[2048]{0:T(1024)S(1)} %bitcast.108, f32[1024]{0:T(1024)S(1)} %bitcast.99, ...), kind=kOutput, calls=%fused_computation.14.clone.1 | convolution fusion | flops 3227516928 | bytes 1597952 | tf_op jit(solution)/shard_map/while/body/eval_jaxpr/dot_general | solution.py:66
  134.2 4.9 %fusion.35 = f32[16,1024,128]{2,1,0:T(8,128)} fusion(f32[16,1024,128]{2,1,0:T(8,128)} %get-tuple-element.297, s32[]{:T(128)} %get-tuple-element.296, f32[2048,128]{1,0:T(8,128)S(1)} %get-tuple-element.315, f32[2048]{0:T(1024)S(1)} %broadcast_bitcast_fusion.2, f32[2048]{0:T(1024)S(1)} %bitcast.108, f32[1024]{0:T(1024)S(1)} %bitcast.99, ...), kind=kOutput, calls=%fused_computation.14.clone.1 | convolution fusion | flops 3227516928 | bytes 1597952 | tf_op jit(solution)/shard_map/while/body/eval_jaxpr/dot_general | solution.py:66
  181.1 4.9 %fusion.35 = f32[16,1024,128]{2,1,0:T(8,128)} fusion(f32[16,1024,128]{2,1,0:T(8,128)} %get-tuple-element.297, s32[]{:T(128)} %get-tuple-element.296, f32[2048,128]{1,0:T(8,128)S(1)} %get-tuple-element.315, f32[2048]{0:T(1024)S(1)} %broadcast_bitcast_fusion.2, f32[2048]{0:T(1024)S(1)} %bitcast.108, f32[1024]{0:T(1024)S(1)} %bitcast.99, ...), kind=kOutput, calls=%fused_computation.14.clone.1 | convolution fusion | flops 3227516928 | bytes 1597952 | tf_op jit(solution)/shard_map/while/body/eval_jaxpr/dot_general | solution.py:66
  190.5 4.9 %fusion.35 = f32[16,1024,128]{2,1,0:T(8,128)} fusion(f32[16,1024,128]{2,1,0:T(8,128)} %get-tuple-element.297, s32[]{:T(128)} %get-tuple-element.296, f32[2048,128]{1,0:T(8,128)S(1)} %get-tuple-element.315, f32[2048]{0:T(1024)S(1)} %broadcast_bitcast_fusion.2, f32[2048]{0:T(1024)S(1)} %bitcast.108, f32[1024]{0:T(1024)S(1)} %bitcast.99, ...), kind=kOutput, calls=%fused_computation.14.clone.1 | convolution fusion | flops 3227516928 | bytes 1597952 | tf_op jit(solution)/shard_map/while/body/eval_jaxpr/dot_general | solution.py:66
  214.2 9.3 %copy.24 = f32[1,16,1,8,128,128]{4,3,5,2,0,1:T(8,128)} copy(f32[1,16,1,8,128,128]{5,4,3,1,2,0:T(8,128)} %bitcast.84) | data formatting | bytes 16777216 | tf_op jit(solution)/shard_map/reshape | solution.py:126
  223.5 5.8 %pad_maximum_fusion = f32[1,16,1,8,128,130]{4,3,5,2,0,1:T(8,128)} fusion(f32[1,16,1,8,128,1]{4,3,5,2,0,1:T(8,128)S(1)} %bitcast.87, f32[1,16,1,8,128,1]{4,3,5,2,0,1:T(8,128)S(1)} %bitcast.86, f32[1,16,1,8,128,128]{4,3,5,2,0,1:T(8,128)} %copy.24), kind=kLoop, calls=%fused_computation.29 | loop fusion | flops 4259840 | bytes 17039360 | tf_op jit(solution)/shard_map/concatenate | solution.py:36
  229.3 6.9 %all-to-all-start.1 = ((f32[1,16,1,8,128,130]{4,3,5,2,0,1:T(8,128)}), f32[1,16,1,8,128,130]{4,3,5,2,0,1:T(8,128)}, u32[]{:S(2)}, u32[]{:S(2)}) async-start(f32[1,16,1,8,128,130]{4,3,5,2,0,1:T(8,128)} %pad_maximum_fusion), calls=%async_computation.1 | async-start | bytes 17039360 | tf_op jit(solution)/shard_map/all_to_all | solution.py:39
  236.2 113.7 %all-to-all-done.1 = f32[1,16,1,8,128,130]{4,3,5,2,0,1:T(8,128)} async-done(((f32[1,16,1,8,128,130]{4,3,5,2,0,1:T(8,128)}), f32[1,16,1,8,128,130]{4,3,5,2,0,1:T(8,128)}, u32[]{:S(2)}, u32[]{:S(2)}) %all-to-all-start.1) | async-done | bytes 8519712 | tf_op jit(solution)/shard_map/all_to_all | solution.py:39
  351.4 7.4 %split.37 = f32[1,1,16,8,128,128]{4,3,5,2,1,0:T(8,128)} slice(f32[1,1,16,8,128,130]{4,3,5,2,1,0:T(8,128)} %bitcast.8), slice={[0:1], [0:1], [0:16], [0:8], [0:128], [0:128]} | slice | bytes 16777216 | tf_op jit(solution)/shard_map/split | solution.py:40
  359.0 31.4 %while.27 = (s32[]{:T(128)}, f32[16,1024,2]{1,2,0:T(2,128)S(1)}, s32[16,1024]{1,0:T(8,128)S(1)}, f32[16,1024,2]{1,2,0:T(2,128)S(1)}, s32[]{:T(128)}) while((s32[]{:T(128)}, f32[16,1024,2]{1,2,0:T(2,128)S(1)}, s32[16,1024]{1,0:T(8,128)S(1)}, f32[16,1024,2]{1,2,0:T(2,128)S(1)}, s32[]{:T(128)}) %tuple.64), condition=%wide.region_3.4_spmd.clone, body=%wide.region_2.3_spmd.clone.sunk | while | flops 26214400 | bytes 29761 | solution.py:108
  390.4 9.3 %copy.23 = f32[1,1,16,8,128,128]{5,4,3,2,1,0:T(8,128)} copy(f32[1,1,16,8,128,128]{4,3,5,2,1,0:T(8,128)} %split.37) | data formatting | bytes 16777216
  399.7 5.3 %all-reduce.5 = (f32[1024]{0:T(1024)S(1)}, f32[1024]{0:T(1024)S(1)}) all-reduce(f32[1024]{0:T(1024)S(1)} %bitcast.105, f32[1024]{0:T(1024)S(1)} %bitcast.104), channel_id=1, replica_groups=mesh['row_0'=2,'row_1'=4,'col_0'=2,'col_1'=4,'col_2'=2] {'row_0'}, use_global_device_ids=true, to_apply=%region_5.6 | all-reduce | flops 2048 | bytes 16384 | tf_op jit(solution)/shard_map/psum | solution.py:48
  405.0 8.3 %all-reduce.2 = (f32[1024]{0:T(1024)S(1)}, f32[1024]{0:T(1024)S(1)}) all-reduce(f32[1024]{0:T(1024)S(1)} %get-tuple-element.176, f32[1024]{0:T(1024)S(1)} %get-tuple-element.177), channel_id=1, replica_groups=mesh['row_0'=2,'row_1'=4,'col_0'=2,'col_1'=4,'col_2'=2] {'row_1'}, use_global_device_ids=true, to_apply=%region_6.7 | all-reduce | flops 2048 | bytes 16384 | tf_op jit(solution)/shard_map/psum | solution.py:48
  417.1 8.3 %all-reduce.1 = (f32[1024]{0:T(1024)S(1)}, f32[1024]{0:T(1024)S(1)}) all-reduce(f32[1024]{0:T(1024)S(1)} %get-tuple-element.174, f32[1024]{0:T(1024)S(1)} %get-tuple-element.175), channel_id=1, replica_groups=mesh['row_0'=2,'row_1'=4,'col_0'=2,'col_1'=4,'col_2'=2] {'col_1'}, use_global_device_ids=true, to_apply=%region_8.9 | all-reduce | flops 2048 | bytes 16384 | tf_op jit(solution)/shard_map/psum | solution.py:48
  425.4 9.4 %all-reduce.3 = (f32[1024]{0:T(1024)S(1)}, f32[1024]{0:T(1024)S(1)}) all-reduce(f32[1024]{0:T(1024)S(1)} %get-tuple-element.168, f32[1024]{0:T(1024)S(1)} %get-tuple-element.169), channel_id=1, replica_groups=mesh['row_0'=2,'row_1'=4,'col_0'=2,'col_1'=4,'col_2'=2] {'col_2'}, use_global_device_ids=true, to_apply=%region_9.10 | all-reduce | flops 2048 | bytes 16384 | tf_op jit(solution)/shard_map/psum | solution.py:48
  (167 shorter events, 152.9 us)
Async XLA Ops:
  7.2 51.9 %all-gather.2.cloned.1.call-start = ((), (), s32[]{:S(2)}) async-start(), calls=%async_computation.2 | async-start | bytes 1198080 | tf_op jit(solution)/shard_map/all_gather | solution.py:27
  12.2 12.9 %all-to-all-start = ((s32[2,1,16,8,128]{4,3,1,0,2:T(8,128)}), s32[2,1,16,8,128]{4,3,1,0,2:T(8,128)S(1)}, u32[]{:S(2)}, u32[]{:S(2)}) async-start(s32[2,1,16,8,128]{4,3,1,0,2:T(8,128)} %pad_add_fusion), calls=%async_computation | async-start | bytes 262144 | tf_op jit(solution)/shard_map/all_to_all | solution.py:18
  229.3 6.9 %copy-start = (s32[1,1,16,8,128]{4,3,2,1,0:T(8,128)S(1)}, s32[1,1,16,8,128]{4,3,2,1,0:T(8,128)}, u32[]{:S(2)}) copy-start(s32[1,1,16,8,128]{4,3,2,1,0:T(8,128)} %param.13) | copy-start | bytes 196612
  229.3 6.9 %copy-start.1 = (s32[1,1,16,8,128]{4,3,2,1,0:T(8,128)S(1)}, s32[1,1,16,8,128]{4,3,2,1,0:T(8,128)}, u32[]{:S(2)}) copy-start(s32[1,1,16,8,128]{4,3,2,1,0:T(8,128)} %param.12) | copy-start | bytes 196612
  229.3 120.6 %all-to-all-start.1 = ((f32[1,16,1,8,128,130]{4,3,5,2,0,1:T(8,128)}), f32[1,16,1,8,128,130]{4,3,5,2,0,1:T(8,128)}, u32[]{:S(2)}, u32[]{:S(2)}) async-start(f32[1,16,1,8,128,130]{4,3,5,2,0,1:T(8,128)} %pad_maximum_fusion), calls=%async_computation.1 | async-start | bytes 17039360 | tf_op jit(solution)/shard_map/all_to_all | solution.py:39
Sparse Core Ops, SparseCore 0:
  10.8 48.1 all-gather.1
where the time goes:
time: 443 us; the launch traced here: 442 us
  matrix products  176 us (40%)
  waiting for transfers between devices  154 us (35%)
  local copies, waits for them, and re-layouts  40.1 us (9%)
  blocking collectives  35.1 us (8%)
  between operations  14.2 us (3%)
  starting transfers between devices  13.7 us (3%)
  other arithmetic  9.45 us (2%)
    all_to_all x1, waiting for transfers between devices, sent_together(): lax.all_to_all(both, axis, split_axis=split_dim, concat_axis=concat_dim,...  114 us
    dot_general x16, matrix products, tile_one_block(): jnp.dot(matched, flat_payload, precision=lax.Precision.HIGHEST, preferred...  78.9 us
    dot_general x16, matrix products, tile_one_block(): jnp.dot(matched, side_columns, precision=lax.Precision.HIGHEST, preferred...  65.6 us
    psum x5, blocking collectives, over_axes(): array = lax.psum(array, axis)  35.1 us
    all_gather x1, waiting for transfers between devices, in_one_piece_2(): whole = lax.all_gather(both, axis, axis=dim, tiled=True)  33.9 us
    dot_general x16, matrix products, partition_one_block(): jnp.dot(onehot, values_here, precision=lax.Precision.HIGHEST, preferred_e...  31 us
    unnamed x8, local copies, waits for them, and re-layouts  9.3 us
    reshape x1, local copies, waits for them, and re-layouts, local(): joined = summed.reshape(1, owners, 1, probe_tiles, tile_rows, columns)  9.26 us
  transfers between devices with their start and end apart: 3, of which 3 were waited for; matrix products, arithmetic and copies ran while one was open for 0% of the time, Pallas kernels for 0%

commit v1 on v0

v1 whole, which is shorter than its diff:
```python
import functools

import jax
import jax.numpy as jnp
from jax import lax
from jax.experimental import pallas as pl
from jax.experimental.pallas import tpu as pltpu
from jax.sharding import Mesh
from jax.sharding import PartitionSpec as P

PARTS_SIZE = 1024
KEYS = 64
ROW = ("row_0", "row_1")
COL = ("col_0", "col_1", "col_2")
ALL = ROW + COL
MESH = pl.DeviceIdType.MESH

PIECE = 136
CUTS = ((0, 48), (48, 48), (96, 40))
ORDERS = ((0, 1, 2), (1, 2, 0), (2, 0, 1))


def table_of(tile_base, key_ref, part_ref, payload_ref):
    lane = lax.broadcasted_iota(jnp.int32, (8, 128), 1)
    sub = lax.broadcasted_iota(jnp.int32, (8, 128), 0)
    keys_col = lax.broadcasted_iota(jnp.int32, (KEYS, 128), 0)
    side_lhs = jnp.where(sub == 0, lane.astype(jnp.float32) / 2048.0, jnp.where(sub == 1, 1.0, 0.0))
    sums, sides = [], []
    for t in range(2):
        onehot = (keys_col == key_ref[0, t : t + 1, :]).astype(jnp.float32)
        sums.append(
            jnp.dot(onehot, payload_ref[0, t], precision=lax.Precision.HIGHEST, preferred_element_type=jnp.float32)
        )
        side = lax.dot_general(
            side_lhs, onehot, (((1,), (1,)), ((), ())), preferred_element_type=jnp.float32
        )
        start = (tile_base + t).astype(jnp.float32) / 16.0
        sides.append(side + jnp.where(sub[:, :KEYS] == 0, start * side[1:2, :], 0.0))
    table = jnp.concatenate(sums, axis=0).T
    side = jnp.concatenate(sides, axis=1)
    for t in range(2):
        side = jnp.where(sub == 2 + t, part_ref[0, t].astype(jnp.float32), side)
    return table, side


def gather_kernel(key_ref, part_ref, payload_ref, g_ref, recv, pair_recv, send):
    yh, z, yl, x, core = (lax.axis_index(a) for a in ALL)
    here = (x, yh * 2 + yl, z)

    def device(at, k):
        return (at[1] // 2, at[2], at[1] % 2, at[0], k)

    def slot(at, k):
        return (((at[1] % 2) * 4 + at[0]) * 2 + k) * 8 + (at[1] // 2) * 4 + at[2]

    def shifted(at, dim, delta):
        return tuple((v + delta) % 4 if d == dim else v for d, v in enumerate(at))

    def place(p, off):
        order = ORDERS[p]
        at = list(here)
        for level in range(3):
            at[order[level]] = (at[order[level]] + off[level]) % 4
        return slot(tuple(at), core)

    def block(p, index):
        return g_ref.at[index, pl.ds(CUTS[p][0], CUTS[p][1])]

    def push(p, off, level, delta):
        far = tuple((o - delta + 4) % 4 if n == level else o for n, o in enumerate(off))
        ref = block(p, place(p, off))
        pltpu.make_async_remote_copy(
            src_ref=ref, dst_ref=ref, send_sem=send.at[p], recv_sem=recv.at[p, far[0] * 16 + far[1] * 4 + far[2]],
            device_id=device(shifted(here, ORDERS[p][level], delta + 4), core), device_id_type=MESH,
        ).start()

    def pair(p, off):
        ref = block(p, place(p, off))
        pltpu.make_async_remote_copy(
            src_ref=ref, dst_ref=ref, send_sem=send.at[p], recv_sem=pair_recv.at[p],
            device_id=device(here, 1 - core), device_id_type=MESH,
        ).start()

    def arrive(p, off):
        ref = block(p, place(p, off))
        pltpu.make_async_remote_copy(
            src_ref=ref, dst_ref=ref, send_sem=send.at[p], recv_sem=recv.at[p, off[0] * 16 + off[1] * 4 + off[2]],
            device_id=device(here, 1 - core), device_id_type=MESH,
        ).wait_recv()

    barrier = pltpu.get_barrier_semaphore()
    for dim in range(3):
        for delta in (1, 3):
            pl.semaphore_signal(barrier, inc=1, device_id=device(shifted(here, dim, delta), core), device_id_type=MESH)
    pl.semaphore_signal(barrier, inc=1, device_id=device(here, 1 - core), device_id_type=MESH)

    table, side = table_of((yh * 4 + z) * 2, key_ref, part_ref, payload_ref)
    own = slot(here, core)
    g_ref[own, :128, :] = table
    g_ref[own, 128:, :] = side
    pl.semaphore_wait(barrier, 7)

    def both(p, off, level):
        push(p, off, level, 1)
        push(p, off, level, -1)

    for level in range(3):
        for p in range(3):
            both(p, (0, 0, 0), level)
    for p in range(3):
        pair(p, (0, 0, 0))
    for p in range(3):
        arrive(p, (3, 0, 0))
        push(p, (3, 0, 0), 0, 1)
    for level in (1, 2):
        for p in range(3):
            both(p, (3, 0, 0), level)
    for p in range(3):
        arrive(p, (1, 0, 0))
        both(p, (1, 0, 0), 1)
        both(p, (1, 0, 0), 2)
    for p in range(3):
        arrive(p, (2, 0, 0))
        both(p, (2, 0, 0), 1)
        both(p, (2, 0, 0), 2)
    for p in range(3):
        for o in (3, 1, 2):
            pair(p, (o, 0, 0))

    def turn(i):
        return i + (i // 2) * (5 - 2 * i)

    def second(i, carry):
        da = turn(i)
        delta = 1 - 2 * (da % 2)
        for p in range(3):
            near = (4 - delta) % 4
            for o in (3, 1):
                arrive(p, (da, o, 0))
                both(p, (da, o, 0), 2)
            push(p, (da, near, 0), 1, delta)
            for o in (3, 1):
                pair(p, (da, o, 0))
        return carry

    def second_far(i, carry):
        da = turn(i)
        for p in range(3):
            arrive(p, (da, 2, 0))
            both(p, (da, 2, 0), 2)
            pair(p, (da, 2, 0))
        return carry

    def third(i, carry):
        da, db = turn(i % 4), turn(i // 4)
        delta = 1 - 2 * ((da + db) % 2)
        near = (4 - delta) % 4
        for p in range(3):
            for o in (3, 1):
                arrive(p, (da, db, o))
            push(p, (da, db, near), 2, delta)
            for o in (3, 1):
                pair(p, (da, db, o))
        return carry

    def third_far(i, carry):
        da, db = turn(i % 4), turn(i // 4)
        for p in range(3):
            arrive(p, (da, db, 2))
            pair(p, (da, db, 2))
        return carry

    lax.fori_loop(0, 4, second, 0)
    lax.fori_loop(0, 4, second_far, 0)
    lax.fori_loop(0, 16, third, 0)
    lax.fori_loop(0, 16, third_far, 0)
    for p in range(3):
        rows = pl.ds(CUTS[p][0], CUTS[p][1])
        landed = g_ref.at[pl.ds(0, 64), rows]
        pltpu.make_async_copy(landed, landed, pair_recv.at[p]).wait()
        sent = g_ref.at[pl.ds(0, 127), rows]
        pltpu.make_async_copy(sent, sent, send.at[p]).wait()


def gather_tables(build_key, build_part, build_payload):
    return pl.pallas_call(
        gather_kernel,
        out_shape=jax.ShapeDtypeStruct((128, PIECE, 128), jnp.float32),
        in_specs=[
            pl.BlockSpec(memory_space=pltpu.VMEM),
            pl.BlockSpec(memory_space=pltpu.SMEM),
            pl.BlockSpec(memory_space=pltpu.VMEM),
        ],
        out_specs=pl.BlockSpec(memory_space=pltpu.VMEM),
        scratch_shapes=[
            pltpu.SemaphoreType.DMA((3, 64)),
            pltpu.SemaphoreType.DMA((3,)),
            pltpu.SemaphoreType.DMA((3,)),
        ],
        compiler_params=pltpu.CompilerParams(
            collective_id=0, has_side_effects=True, vmem_limit_bytes=16 * 1024 * 1024
        ),
        name="gather_tables",
    )(build_key, build_part, build_payload)


def join_kernel(key_ref, part_ref, g_ref, joined_ref, place_ref, stat_ref, table, hot, same):
    @pl.when(pl.program_id(0) == 0)
    def _():
        stat_ref[...] = jnp.zeros_like(stat_ref)

    keys = key_ref[0]
    parts = part_ref[0]
    parts_f = parts.astype(jnp.float32)
    for r in range(8):
        piece = g_ref[r]
        high = piece.astype(jnp.bfloat16)
        low = (piece - high.astype(jnp.float32)).astype(jnp.bfloat16)
        lanes = pl.ds(r * 128, 128)
        table[0:128, lanes] = high[:128]
        table[128:256, lanes] = low[:128]
        table[256:272, lanes] = jnp.concatenate(
            [high[128:].astype(jnp.float32), low[128:].astype(jnp.float32)], axis=0
        ).astype(jnp.bfloat16)
        for t in range(2):
            same[r * 2 + t] = (parts_f == piece[130 + t : 131 + t, :]).astype(jnp.float32)
    key_col = lax.broadcasted_iota(jnp.int32, (KEYS, 128), 0)
    counts = []
    for q2 in range(4):
        for h in range(2):
            q = q2 * 2 + h
            key_hot = (key_col == keys[q : q + 1, :]).astype(jnp.float32).astype(jnp.bfloat16)
            lanes = pl.ds(h * 128, 128)
            for t in range(16):
                row = jnp.broadcast_to(same[t, q : q + 1, :], (16, 128)).astype(jnp.bfloat16)
                hot[q2, t * KEYS : (t + 1) * KEYS, lanes] = key_hot * jnp.concatenate([row] * 4, axis=0)
        out = jnp.dot(table[...], hot[q2], preferred_element_type=jnp.float32)
        sums = out[:128] + out[128:256]
        joined_ref[0, q2 * 2] = sums[:, :128].T
        joined_ref[0, q2 * 2 + 1] = sums[:, 128:].T
        side = out[256:264] + out[264:272]
        for h in range(2):
            place_ref[0, q2 * 2 + h : q2 * 2 + h + 1, :] = side[0:1, h * 128 : (h + 1) * 128]
            counts.append(side[1:2, h * 128 : (h + 1) * 128])

    count = jnp.concatenate(counts, axis=0)
    count_high = jnp.floor(count * (1.0 / 64.0))
    count_low = count - 64.0 * count_high
    live = (keys >= 0).astype(jnp.float32)
    major = parts // 128
    minor = parts - major * 128
    sub8 = lax.broadcasted_iota(jnp.int32, (8, 128), 0)
    sub128 = lax.broadcasted_iota(jnp.int32, (128, 128), 0)
    total = jnp.zeros((32, 128), jnp.float32)
    for q in range(8):
        major_hot = sub8 == major[q : q + 1, :]
        lhs = jnp.concatenate(
            [
                jnp.where(major_hot, v[q : q + 1, :], 0.0)
                for v in (count_high, count_low, live, jnp.zeros_like(live))
            ],
            axis=0,
        ).astype(jnp.bfloat16)
        rhs = (sub128 == minor[q : q + 1, :]).astype(jnp.float32).astype(jnp.bfloat16)
        total += lax.dot_general(lhs, rhs, (((1,), (1,)), ((), ())), preferred_element_type=jnp.float32)
    stat_ref[0:8, :] += 64.0 * total[0:8] + total[8:16]
    stat_ref[8:16, :] += total[16:24]


def join(probe_key, probe_part, tables):
    return pl.pallas_call(
        join_kernel,
        grid=(16,),
        out_shape=(
            jax.ShapeDtypeStruct((16, 8, 128, 128), jnp.float32),
            jax.ShapeDtypeStruct((16, 8, 128), jnp.float32),
            jax.ShapeDtypeStruct((16, 128), jnp.float32),
        ),
        in_specs=[
            pl.BlockSpec((1, 8, 128), lambda c: (c, 0, 0)),
            pl.BlockSpec((1, 8, 128), lambda c: (c, 0, 0)),
            pl.BlockSpec((8, PIECE, 128), lambda c: (c, 0, 0)),
        ],
        out_specs=(
            pl.BlockSpec((1, 8, 128, 128), lambda c: (c, 0, 0, 0)),
            pl.BlockSpec((1, 8, 128), lambda c: (c, 0, 0)),
            pl.BlockSpec((16, 128), lambda c: (0, 0)),
        ),
        scratch_shapes=[
            pltpu.VMEM((272, 1024), jnp.bfloat16),
            pltpu.VMEM((4, 1024, 256), jnp.bfloat16),
            pltpu.VMEM((16, 8, 128), jnp.float32),
        ],
        compiler_params=pltpu.CompilerParams(vmem_limit_bytes=32 * 1024 * 1024),
        name="join",
    )(probe_key, probe_part, tables)


def local(build_key, build_part, build_payload, probe_key, probe_part):
    tables = gather_tables(build_key, build_part, build_payload)
    joined, places, stats = join(probe_key.reshape(16, 8, 128), probe_part.reshape(16, 8, 128), tables)
    stats = lax.psum(stats, ALL)
    rate = stats[:8].reshape(PARTS_SIZE) / jnp.maximum(stats[8:].reshape(PARTS_SIZE), 1.0)
    return (joined[None, None], places[None, None], rate)


def solution(mesh):
    finer = Mesh(mesh.devices.reshape(2, 4, 2, 4, 2), ALL)
    return jax.shard_map(
        local,
        mesh=finer,
        in_specs=(
            P(COL, ROW, None),
            P(COL, ROW),
            P(COL, ROW, None, None),
            P(ROW, COL, None, None, None),
            P(ROW, COL, None, None, None),
        ),
        out_specs=(P(ROW, COL, None, None, None, None), P(ROW, COL, None, None, None), P()),
        check_vma=False,
    )
```

time: 443 us -> 118 us (0.27)
  matrix products: 176 us -> 0 us
  waiting for transfers between devices: 154 us -> 0 us
  Pallas kernels: 0 us -> 51.8 us
  local copies, waits for them, and re-layouts: 40.1 us -> 2.24 us
  blocking collectives: 35.1 us -> 62.4 us
  starting transfers between devices: 13.7 us -> 0 us
  between operations: 14.2 us -> 0.67 us
  other arithmetic: 9.45 us -> 0.6 us
    dot_general x48 -> x0, matrix products: 176 us -> none  [the longest x16 78.9 us: tile_one_block(): jnp.dot(matched, flat_payload, precision=lax.Precision.HIGHEST, preferred...]
    all_to_all x2 -> x0, waiting for transfers between devices: 120 us -> none  [the longest x1 114 us: sent_together(): lax.all_to_all(both, axis, split_axis=split_dim, concat_axis=concat_dim,...]
    pallas_call x0 -> x2, Pallas kernels: none -> 51.8 us  [the longest x1 33.6 us: gather_tables(): pl.pallas_call(gather_kernel, out_shape=jax.ShapeDtypeStruct((128, PIECE,...]
    all_gather x1 -> x0, waiting for transfers between devices: 33.9 us -> none  [in_one_piece_2(): whole = lax.all_gather(both, axis, axis=dim, tiled=True)]
    psum x5 -> x1, blocking collectives: 35.1 us -> 62.4 us  [local(): stats = lax.psum(stats, ALL)]
    split x5 -> x0, local copies, waits for them, and re-layouts: 14 us -> none  [the longest x2 8.93 us: sent_together(): jnp.split(whole, [sum(widths[:k]) for k in range(1, len(widths))], axis=a...]
    all_to_all x2 -> x0, starting transfers between devices: 13.7 us -> none  [the longest x1 6.87 us: sent_together(): lax.all_to_all(both, axis, split_axis=split_dim, concat_axis=concat_dim,...]
    reshape x2 -> x0, local copies, waits for them, and re-layouts: 9.36 us -> none  [the longest x1 9.26 us: local(): joined = summed.reshape(1, owners, 1, probe_tiles, tile_rows, columns)]
  transfers between devices with their start and end apart: 3 -> 0, of which waited for: 3 -> 0; matrix products, arithmetic and copies ran while one was open for 0% -> 0% of each run, Pallas kernels for 0% -> 0%
where the time goes in v1:
time: 118 us
  blocking collectives  62.4 us (53%)
  Pallas kernels  51.8 us (44%)
  local copies, waits for them, and re-layouts  2.24 us (2%)
    psum x1, blocking collectives, local(): stats = lax.psum(stats, ALL)  62.4 us
    pallas_call x1, Pallas kernels, gather_tables(): pl.pallas_call(gather_kernel, out_shape=jax.ShapeDtypeStruct((128, PIECE,...  33.6 us
    pallas_call x1, Pallas kernels, join(): pl.pallas_call(join_kernel, grid=(16,), out_shape=(jax.ShapeDtypeStruct((...  18.1 us

profile of v1, /device:TPU:1, one launch (start us, length us, event | category | flops | bytes accessed | tf_op | source)
XLA Modules:
  0.0 117.7 jit_solution(13497201700380803872)
XLA Ops:
  0.6 0.0 copy-start
  0.6 0.9 copy-done
  1.5 0.0 copy-start.3
  1.5 0.7 copy-done.3
  2.2 0.0 copy-start.4
  2.2 0.7 copy-done.4
  2.9 0.0 copy-start.1
  2.9 0.0 copy-start.2
  2.9 33.6 %gather_tables.1.g_ref = f32[128,136,128]{2,1,0:T(8,128)S(1)} custom-call(s32[1,2,128]{2,1,0:T(2,128)S(1)} %copy-done.3, s32[1,2]{1,0:T(1,128)S(1)} %copy-done.4, f32[1,2,128,128]{3,2,1,0:T(8,128)S(1)} %copy-done), custom_call_target="tpu_custom_call" | custom-call | tf_op jit(solution)/shard_map/gather_tables/pallas_call | solution.py:186
  36.5 0.0 copy-done.1
  36.5 0.0 copy-done.2
  36.5 18.1 %join.1 = (f32[16,8,128,128]{3,2,1,0:T(8,128)}, f32[16,8,128]{2,1,0:T(8,128)}, f32[16,128]{1,0:T(8,128)S(1)}) custom-call(s32[16,8,128]{2,1,0:T(8,128)S(1)} %bitcast.6, s32[16,8,128]{2,1,0:T(8,128)S(1)} %bitcast.7, f32[128,136,128]{2,1,0:T(8,128)S(1)} %gather_tables.1.g_ref), custom_call_target="tpu_custom_call" | custom-call | tf_op jit(solution)/shard_map/join/pallas_call | solution.py:271
  54.7 62.4 %psum.7 = f32[16,128]{1,0:T(8,128)S(1)} all-reduce(f32[16,128]{1,0:T(8,128)S(1)} %get-tuple-element.8), channel_id=1, replica_groups=mesh['row_0'=2,'row_1'=4,'col_0'=2,'col_1'=4,'col_2'=2] {'row_0','row_1'..., use_global_device_ids=true, to_apply=%region_0.0 | all-reduce | flops 2048 | bytes 16384 | tf_op jit(solution)/shard_map/psum | solution.py:302
  117.1 0.6 fusion.1
Async XLA Ops:
  0.6 0.9 copy-start
  1.5 0.7 copy-start.3
  2.2 0.7 copy-start.4
  2.9 33.6 %copy-start.1 = (s32[1,1,16,8,128]{4,3,2,1,0:T(8,128)S(1)}, s32[1,1,16,8,128]{4,3,2,1,0:T(8,128)}, u32[]{:S(2)}) copy-start(s32[1,1,16,8,128]{4,3,2,1,0:T(8,128)} %param.8) | copy-start | bytes 196612
  2.9 33.7 %copy-start.2 = (s32[1,1,16,8,128]{4,3,2,1,0:T(8,128)S(1)}, s32[1,1,16,8,128]{4,3,2,1,0:T(8,128)}, u32[]{:S(2)}) copy-start(s32[1,1,16,8,128]{4,3,2,1,0:T(8,128)} %param.9) | copy-start | bytes 196612

commit v2 on v1

--- a/solution.py
+++ b/solution.py
@@ -18,6 +18,11 @@
 PIECE = 136
 CUTS = ((0, 48), (48, 48), (96, 40))
 ORDERS = ((0, 1, 2), (1, 2, 0), (2, 0, 1))
+
+
+def coded(part):
+    major = part // 128
+    return (128 + part - major * 128).astype(jnp.float32) * (1 << major).astype(jnp.float32)
 
 
 def table_of(tile_base, key_ref, part_ref, payload_ref):
@@ -39,12 +44,80 @@
     table = jnp.concatenate(sums, axis=0).T
     side = jnp.concatenate(sides, axis=1)
     for t in range(2):
-        side = jnp.where(sub == 2 + t, part_ref[0, t].astype(jnp.float32), side)
+        part = part_ref[0, t]
+        side = jnp.where(sub == 2 + t, part.astype(jnp.float32), side)
+        side = jnp.where(sub == 4 + t, coded(jnp.full((8, 128), part)), side)
     return table, side
 
 
-def gather_kernel(key_ref, part_ref, payload_ref, g_ref, recv, pair_recv, send):
+def live_rows(key_ref, part_ref):
+    sub8 = lax.broadcasted_iota(jnp.int32, (8, 128), 0)
+    sub128 = lax.broadcasted_iota(jnp.int32, (128, 128), 0)
+
+    def column(c, total):
+        keys, parts = key_ref[c], part_ref[c]
+        major = parts // 128
+        minor = parts - major * 128
+        lhs, rhs = [], []
+        for q in range(8):
+            live = (sub8 == major[q : q + 1, :]) & (keys[q : q + 1, :] >= 0)
+            lhs.append(jnp.where(live, 1.0, 0.0))
+            rhs.append((sub128 == minor[q : q + 1, :]).astype(jnp.float32).astype(jnp.bfloat16))
+        lhs = jnp.concatenate(lhs, axis=1).astype(jnp.bfloat16)
+        rhs = jnp.concatenate(rhs, axis=1)
+        return total + lax.dot_general(lhs, rhs, (((1,), (1,)), ((), ())), preferred_element_type=jnp.float32)
+
+    return lax.fori_loop(0, 16, column, jnp.zeros((8, 128), jnp.float32))
+
+
+def match_rows(key_ref, part_ref, g_ref):
+    sub8 = lax.broadcasted_iota(jnp.int32, (8, 128), 0)
+    lane8 = lax.broadcasted_iota(jnp.int32, (8, 128), 1)
+    label = (sub8 * 128 + lane8).astype(jnp.float32)
+    first = lane8 < KEYS
+    sub128 = lax.broadcasted_iota(jnp.int32, (128, 128), 0)
+    key_at = jnp.where(sub128 >= KEYS, sub128 - KEYS, sub128)
+
+    def column(c, total):
+        keys, parts = key_ref[c], part_ref[c].astype(jnp.float32)
+        pieces = pl.ds(c * 8, 8)
+        count, even, odd = g_ref[pieces, 129, :], g_ref[pieces, 130, :], g_ref[pieces, 131, :]
+        lhs, rhs = [], []
+        for q in range(8):
+            row = parts[q : q + 1, :]
+            lhs.append(jnp.concatenate([jnp.where(even == row, 1.0, 0.0), jnp.where(odd == row, 1.0, 0.0)], axis=0))
+            rhs.append((key_at == keys[q : q + 1, :]).astype(jnp.float32).astype(jnp.bfloat16))
+        lhs = jnp.concatenate(lhs, axis=1).astype(jnp.bfloat16)
+        rhs = jnp.concatenate(rhs, axis=1)
+        seen = lax.dot_general(lhs, rhs, (((1,), (1,)), ((), ())), preferred_element_type=jnp.float32)
+        pairs = jnp.where(first, seen[:8], seen[8:]) * count
+        left = jnp.sum(jnp.where(first, pairs, 0.0), axis=1, keepdims=True)
+        right = jnp.sum(jnp.where(first, 0.0, pairs), axis=1, keepdims=True)
+        for r in range(8):
+            total = total + jnp.where(label == even[r : r + 1, :], left[r : r + 1, :], 0.0)
+            total = total + jnp.where(label == odd[r : r + 1, :], right[r : r + 1, :], 0.0)
+        return total
+
+    return lax.fori_loop(0, 16, column, jnp.zeros((8, 128), jnp.float32))
+
+
+def gather_kernel(
+    key_hbm, part_hbm, payload_hbm, probe_key_hbm, probe_part_hbm, g_ref, stat_ref,
+    key_ref, part_ref, payload_ref, probe_key, probe_part, sums, parcels,
+    loads, recv, pair_recv, send, stat_send, stat_recv,
+):
     yh, z, yl, x, core = (lax.axis_index(a) for a in ALL)
+    incoming = [
+        pltpu.make_async_copy(src, dst, loads.at[n])
+        for n, (src, dst) in enumerate(
+            (
+                (key_hbm, key_ref), (part_hbm, part_ref), (payload_hbm, payload_ref),
+                (probe_key_hbm, probe_key), (probe_part_hbm, probe_part),
+            )
+        )
+    ]
+    for copy in incoming:
+        copy.start()
     here = (x, yh * 2 + yl, z)
 
     def device(at, k):
@@ -94,6 +167,8 @@
             pl.semaphore_signal(barrier, inc=1, device_id=device(shifted(here, dim, delta), core), device_id_type=MESH)
     pl.semaphore_signal(barrier, inc=1, device_id=device(here, 1 - core), device_id_type=MESH)
 
+    for copy in incoming[:3]:
+        copy.wait()
     table, side = table_of((yh * 4 + z) * 2, key_ref, part_ref, payload_ref)
     own = slot(here, core)
     g_ref[own, :128, :] = table
@@ -109,6 +184,9 @@
             both(p, (0, 0, 0), level)
     for p in range(3):
         pair(p, (0, 0, 0))
+    for copy in incoming[3:]:
+        copy.wait()
+    live = live_rows(probe_key, probe_part)
     for p in range(3):
         arrive(p, (3, 0, 0))
         push(p, (3, 0, 0), 0, 1)
@@ -178,40 +256,71 @@
         rows = pl.ds(CUTS[p][0], CUTS[p][1])
         landed = g_ref.at[pl.ds(0, 64), rows]
         pltpu.make_async_copy(landed, landed, pair_recv.at[p]).wait()
+
+    now = jnp.concatenate([match_rows(probe_key, probe_part, g_ref), live], axis=0)
+    first = 0
+    for phase in range(4):
+        sums[phase] = now
+        sent = []
+        for n in range(1 if phase == 0 else 3):
+            target = device(here, 1 - core) if phase == 0 else device(shifted(here, phase - 1, n + 1), core)
+            sent.append(
+                pltpu.make_async_remote_copy(
+                    src_ref=sums.at[phase], dst_ref=parcels.at[first + n], send_sem=stat_send.at[first + n],
+                    recv_sem=stat_recv.at[first + n], device_id=target, device_id_type=MESH,
+                )
+            )
+            sent[-1].start()
+        for n, copy in enumerate(sent):
+            copy.wait_recv()
+            now = now + parcels[first + n]
+        for copy in sent:
+            copy.wait_send()
+        first += len(sent)
+    stat_ref[...] = now
+    for p in range(3):
+        rows = pl.ds(CUTS[p][0], CUTS[p][1])
         sent = g_ref.at[pl.ds(0, 127), rows]
         pltpu.make_async_copy(sent, sent, send.at[p]).wait()
 
 
-def gather_tables(build_key, build_part, build_payload):
+def gather_tables(build_key, build_part, build_payload, probe_key, probe_part):
+    hbm = pl.BlockSpec(memory_space=pltpu.HBM)
+    vmem = pl.BlockSpec(memory_space=pltpu.VMEM)
     return pl.pallas_call(
         gather_kernel,
-        out_shape=jax.ShapeDtypeStruct((128, PIECE, 128), jnp.float32),
-        in_specs=[
-            pl.BlockSpec(memory_space=pltpu.VMEM),
-            pl.BlockSpec(memory_space=pltpu.SMEM),
-            pl.BlockSpec(memory_space=pltpu.VMEM),
-        ],
-        out_specs=pl.BlockSpec(memory_space=pltpu.VMEM),
+        out_shape=(
+            jax.ShapeDtypeStruct((128, PIECE, 128), jnp.float32),
+            jax.ShapeDtypeStruct((16, 128), jnp.float32),
+        ),
+        in_specs=[hbm] * 5,
+        out_specs=(vmem, vmem),
         scratch_shapes=[
+            pltpu.VMEM((1, 2, 128), jnp.int32),
+            pltpu.SMEM((1, 2), jnp.int32),
+            pltpu.VMEM((1, 2, 128, 128), jnp.float32),
+            pltpu.VMEM((16, 8, 128), jnp.int32),
+            pltpu.VMEM((16, 8, 128), jnp.int32),
+            pltpu.VMEM((4, 16, 128), jnp.float32),
+            pltpu.VMEM((10, 16, 128), jnp.float32),
+            pltpu.SemaphoreType.DMA((5,)),
             pltpu.SemaphoreType.DMA((3, 64)),
             pltpu.SemaphoreType.DMA((3,)),
             pltpu.SemaphoreType.DMA((3,)),
+            pltpu.SemaphoreType.DMA((10,)),
+            pltpu.SemaphoreType.DMA((10,)),
         ],
         compiler_params=pltpu.CompilerParams(
             collective_id=0, has_side_effects=True, vmem_limit_bytes=16 * 1024 * 1024
         ),
         name="gather_tables",
-    )(build_key, build_part, build_payload)
-
-
-def join_kernel(key_ref, part_ref, g_ref, joined_ref, place_ref, stat_ref, table, hot, same):
-    @pl.when(pl.program_id(0) == 0)
-    def _():
-        stat_ref[...] = jnp.zeros_like(stat_ref)
-
-    keys = key_ref[0]
-    parts = part_ref[0]
-    parts_f = parts.astype(jnp.float32)
+    )(build_key, build_part, build_payload, probe_key, probe_part)
+
+
+def join_kernel(key_ref, part_ref, g_ref, joined_ref, place_ref, table, hot):
+    keys = key_ref[0].astype(jnp.float32)
+    codes = coded(part_ref[0])
+    tiles = []
     for r in range(8):
         piece = g_ref[r]
         high = piece.astype(jnp.bfloat16)
@@ -223,17 +332,19 @@
             [high[128:].astype(jnp.float32), low[128:].astype(jnp.float32)], axis=0
         ).astype(jnp.bfloat16)
         for t in range(2):
-            same[r * 2 + t] = (parts_f == piece[130 + t : 131 + t, :]).astype(jnp.float32)
-    key_col = lax.broadcasted_iota(jnp.int32, (KEYS, 128), 0)
-    counts = []
+            tiles.append(jnp.broadcast_to(piece[132 + t : 133 + t, :], (16, 128)).astype(jnp.bfloat16))
+    numbers = lax.broadcasted_iota(jnp.int32, (KEYS, 128), 0).astype(jnp.float32).astype(jnp.bfloat16)
+    one, none = jnp.ones((KEYS, 128), jnp.bfloat16), jnp.zeros((KEYS, 128), jnp.bfloat16)
     for q2 in range(4):
         for h in range(2):
             q = q2 * 2 + h
-            key_hot = (key_col == keys[q : q + 1, :]).astype(jnp.float32).astype(jnp.bfloat16)
+            key_row = jnp.broadcast_to(keys[q : q + 1, :], (16, 128)).astype(jnp.bfloat16)
+            key_hot = jnp.where(jnp.concatenate([key_row] * 4, axis=0) == numbers, one, none)
+            code = jnp.broadcast_to(codes[q : q + 1, :], (16, 128)).astype(jnp.bfloat16)
             lanes = pl.ds(h * 128, 128)
             for t in range(16):
-                row = jnp.broadcast_to(same[t, q : q + 1, :], (16, 128)).astype(jnp.bfloat16)
-                hot[q2, t * KEYS : (t + 1) * KEYS, lanes] = key_hot * jnp.concatenate([row] * 4, axis=0)
+                same = jnp.where(code == tiles[t], one[:16], none[:16])
+                hot[q2, t * KEYS : (t + 1) * KEYS, lanes] = key_hot * jnp.concatenate([same] * 4, axis=0)
         out = jnp.dot(table[...], hot[q2], preferred_element_type=jnp.float32)
         sums = out[:128] + out[128:256]
         joined_ref[0, q2 * 2] = sums[:, :128].T
@@ -241,30 +352,6 @@
         side = out[256:264] + out[264:272]
         for h in range(2):
             place_ref[0, q2 * 2 + h : q2 * 2 + h + 1, :] = side[0:1, h * 128 : (h + 1) * 128]
-            counts.append(side[1:2, h * 128 : (h + 1) * 128])
-
-    count = jnp.concatenate(counts, axis=0)
-    count_high = jnp.floor(count * (1.0 / 64.0))
-    count_low = count - 64.0 * count_high
-    live = (keys >= 0).astype(jnp.float32)
-    major = parts // 128
-    minor = parts - major * 128
-    sub8 = lax.broadcasted_iota(jnp.int32, (8, 128), 0)
-    sub128 = lax.broadcasted_iota(jnp.int32, (128, 128), 0)
-    total = jnp.zeros((32, 128), jnp.float32)
-    for q in range(8):
-        major_hot = sub8 == major[q : q + 1, :]
-        lhs = jnp.concatenate(
-            [
-                jnp.where(major_hot, v[q : q + 1, :], 0.0)
-                for v in (count_high, count_low, live, jnp.zeros_like(live))
-            ],
-            axis=0,
-        ).astype(jnp.bfloat16)
-        rhs = (sub128 == minor[q : q + 1, :]).astype(jnp.float32).astype(jnp.bfloat16)
-        total += lax.dot_general(lhs, rhs, (((1,), (1,)), ((), ())), preferred_element_type=jnp.float32)
-    stat_ref[0:8, :] += 64.0 * total[0:8] + total[8:16]
-    stat_ref[8:16, :] += total[16:24]
 
 
 def join(probe_key, probe_part, tables):
@@ -274,7 +361,6 @@
         out_shape=(
             jax.ShapeDtypeStruct((16, 8, 128, 128), jnp.float32),
             jax.ShapeDtypeStruct((16, 8, 128), jnp.float32),
-            jax.ShapeDtypeStruct((16, 128), jnp.float32),
         ),
         in_specs=[
             pl.BlockSpec((1, 8, 128), lambda c: (c, 0, 0)),
@@ -284,12 +370,10 @@
         out_specs=(
             pl.BlockSpec((1, 8, 128, 128), lambda c: (c, 0, 0, 0)),
             pl.BlockSpec((1, 8, 128), lambda c: (c, 0, 0)),
-            pl.BlockSpec((16, 128), lambda c: (0, 0)),
         ),
         scratch_shapes=[
             pltpu.VMEM((272, 1024), jnp.bfloat16),
             pltpu.VMEM((4, 1024, 256), jnp.bfloat16),
-            pltpu.VMEM((16, 8, 128), jnp.float32),
         ],
         compiler_params=pltpu.CompilerParams(vmem_limit_bytes=32 * 1024 * 1024),
         name="join",
@@ -297,9 +381,9 @@
 
 
 def local(build_key, build_part, build_payload, probe_key, probe_part):
-    tables = gather_tables(build_key, build_part, build_payload)
-    joined, places, stats = join(probe_key.reshape(16, 8, 128), probe_part.reshape(16, 8, 128), tables)
-    stats = lax.psum(stats, ALL)
+    probe_key, probe_part = probe_key.reshape(16, 8, 128), probe_part.reshape(16, 8, 128)
+    tables, stats = gather_tables(build_key, build_part, build_payload, probe_key, probe_part)
+    joined, places = join(probe_key, probe_part, tables)
     rate = stats[:8].reshape(PARTS_SIZE) / jnp.maximum(stats[8:].reshape(PARTS_SIZE), 1.0)
     return (joined[None, None], places[None, None], rate)
 

time: 118 us -> 70.6 us (0.60)
  the two profiles are of different devices: /device:TPU:1 before, /device:TPU:0 now
where the time goes in v2:
time: 70.6 us; the launch traced here: 70.3 us
  Pallas kernels  63.4 us (90%)
  local copies, waits for them, and re-layouts  5.58 us (8%)
    pallas_call x1, Pallas kernels, gather_tables(): pl.pallas_call(gather_kernel, out_shape=(jax.ShapeDtypeStruct((128, PIECE...  47.3 us
    pallas_call x1, Pallas kernels, join(): pl.pallas_call(join_kernel, grid=(16,), out_shape=(jax.ShapeDtypeStruct((...  16.1 us
    unnamed x14, local copies, waits for them, and re-layouts  5.58 us

profile of v2, /device:TPU:0, one launch (start us, length us, event | category | flops | bytes accessed | tf_op | source)
XLA Modules:
  0.0 70.3 jit_solution(1361395981033899757)
XLA Ops:
  0.6 0.0 copy-start
  0.6 0.8 %copy-done = s32[1,1,16,8,128]{4,3,2,1,0:T(8,128)S(1)} copy-done((s32[1,1,16,8,128]{4,3,2,1,0:T(8,128)S(1)}, s32[1,1,16,8,128]{4,3,2,1,0:T(8,128)}, u32[]{:S(2)}) %copy-start) | copy-done | bytes 65560
  1.5 0.0 copy-start.2
  1.5 0.8 %copy-done.2 = s32[1,1,16,8,128]{4,3,2,1,0:T(8,128)S(1)} copy-done((s32[1,1,16,8,128]{4,3,2,1,0:T(8,128)S(1)}, s32[1,1,16,8,128]{4,3,2,1,0:T(8,128)}, u32[]{:S(2)}) %copy-start.2) | copy-done | bytes 65560
  2.3 0.0 copy-start.4
  2.3 0.9 %copy-done.4 = f32[1,2,128,128]{3,2,1,0:T(8,128)S(1)} copy-done((f32[1,2,128,128]{3,2,1,0:T(8,128)S(1)}, f32[1,2,128,128]{3,2,1,0:T(8,128)}, u32[]{:S(2)}) %copy-start.4) | copy-done | bytes 131096
  3.2 0.0 copy-start.5
  3.2 0.7 copy-done.5
  3.9 0.0 copy-start.6
  3.9 0.7 copy-done.6
  4.6 47.3 %gather_tables.1 = (f32[128,136,128]{2,1,0:T(8,128)S(1)}, f32[16,128]{1,0:T(8,128)S(1)}) custom-call(s32[1,2,128]{2,1,0:T(2,128)S(1)} %copy-done.5, s32[1,2]{1,0:T(1,128)S(1)} %copy-done.6, f32[1,2,128,128]{3,2,1,0:T(8,128)S(1)} %copy-done.4, s32[16,8,128]{2,1,0:T(8,128)S(1)} %bitcast.6, s32[16,8,128]{2,1,0:T(8,128)S(1)} %bitcast.8), custom_call_target="tpu_custom_call" | custom-call | tf_op jit(solution)/shard_map/gather_tables/pallas_call | solution.py:290
  51.8 0.0 copy-start.1
  51.8 0.8 %copy-done.1 = s32[1,1,16,8,128]{4,3,2,1,0:T(8,128)S(1)} copy-done((s32[1,1,16,8,128]{4,3,2,1,0:T(8,128)S(1)}, s32[1,1,16,8,128]{4,3,2,1,0:T(8,128)}, u32[]{:S(2)}) %copy-start.1) | copy-done | bytes 65560
  52.7 0.0 copy-start.3
  52.7 0.8 %copy-done.3 = s32[1,1,16,8,128]{4,3,2,1,0:T(8,128)S(1)} copy-done((s32[1,1,16,8,128]{4,3,2,1,0:T(8,128)S(1)}, s32[1,1,16,8,128]{4,3,2,1,0:T(8,128)}, u32[]{:S(2)}) %copy-start.3) | copy-done | bytes 65560
  53.5 16.1 %join.1 = (f32[16,8,128,128]{3,2,1,0:T(8,128)}, f32[16,8,128]{2,1,0:T(8,128)}) custom-call(s32[16,8,128]{2,1,0:T(8,128)S(1)} %bitcast.7, s32[16,8,128]{2,1,0:T(8,128)S(1)} %bitcast.9, f32[128,136,128]{2,1,0:T(8,128)S(1)} %get-tuple-element.7.g_ref), custom_call_target="tpu_custom_call" | custom-call | tf_op jit(solution)/shard_map/join/pallas_call | solution.py:358
  69.7 0.6 divide_bitcast_fusion
Async XLA Ops:
  0.6 0.8 %copy-start = (s32[1,1,16,8,128]{4,3,2,1,0:T(8,128)S(1)}, s32[1,1,16,8,128]{4,3,2,1,0:T(8,128)}, u32[]{:S(2)}) copy-start(s32[1,1,16,8,128]{4,3,2,1,0:T(8,128)} %param.8) | copy-start | bytes 196612
  1.5 0.8 %copy-start.2 = (s32[1,1,16,8,128]{4,3,2,1,0:T(8,128)S(1)}, s32[1,1,16,8,128]{4,3,2,1,0:T(8,128)}, u32[]{:S(2)}) copy-start(s32[1,1,16,8,128]{4,3,2,1,0:T(8,128)} %param.9) | copy-start | bytes 196612
  2.3 0.9 %copy-start.4 = (f32[1,2,128,128]{3,2,1,0:T(8,128)S(1)}, f32[1,2,128,128]{3,2,1,0:T(8,128)}, u32[]{:S(2)}) copy-start(f32[1,2,128,128]{3,2,1,0:T(8,128)} %payload_hbm.1) | copy-start | bytes 393220
  3.2 0.7 copy-start.5
  3.9 0.7 copy-start.6
  51.8 0.8 %copy-start.1 = (s32[1,1,16,8,128]{4,3,2,1,0:T(8,128)S(1)}, s32[1,1,16,8,128]{4,3,2,1,0:T(8,128)}, u32[]{:S(2)}) copy-start(s32[1,1,16,8,128]{4,3,2,1,0:T(8,128)} %param.8) | copy-start | bytes 196612
  52.7 0.8 %copy-start.3 = (s32[1,1,16,8,128]{4,3,2,1,0:T(8,128)S(1)}, s32[1,1,16,8,128]{4,3,2,1,0:T(8,128)}, u32[]{:S(2)}) copy-start(s32[1,1,16,8,128]{4,3,2,1,0:T(8,128)} %param.9) | copy-start | bytes 196612

commit v3 on v2

--- a/solution.py
+++ b/solution.py
@@ -67,7 +67,12 @@
         rhs = jnp.concatenate(rhs, axis=1)
         return total + lax.dot_general(lhs, rhs, (((1,), (1,)), ((), ())), preferred_element_type=jnp.float32)
 
-    return lax.fori_loop(0, 16, column, jnp.zeros((8, 128), jnp.float32))
+    def columns(i, total):
+        for n in range(4):
+            total = column(i * 4 + n, total)
+        return total
+
+    return lax.fori_loop(0, 4, columns, jnp.zeros((8, 128), jnp.float32))
 
 
 def match_rows(key_ref, part_ref, g_ref):
@@ -98,12 +103,58 @@
             total = total + jnp.where(label == odd[r : r + 1, :], right[r : r + 1, :], 0.0)
         return total
 
-    return lax.fori_loop(0, 16, column, jnp.zeros((8, 128), jnp.float32))
+    def columns(i, total):
+        for n in range(4):
+            total = column(i * 4 + n, total)
+        return total
+
+    return lax.fori_loop(0, 4, columns, jnp.zeros((8, 128), jnp.float32))
+
+
+def prepare(c, key_ref, part_ref, g_ref, table, hot):
+    keys = key_ref[c].astype(jnp.float32)
+    codes = coded(part_ref[c])
+    tiles = []
+    for r in range(8):
+        piece = g_ref[c * 8 + r]
+        high = piece.astype(jnp.bfloat16)
+        low = (piece - high.astype(jnp.float32)).astype(jnp.bfloat16)
+        lanes = pl.ds(r * 128, 128)
+        table[0:128, lanes] = high[:128]
+        table[128:256, lanes] = low[:128]
+        table[256:272, lanes] = jnp.concatenate(
+            [high[128:].astype(jnp.float32), low[128:].astype(jnp.float32)], axis=0
+        ).astype(jnp.bfloat16)
+        for t in range(2):
+            tiles.append(jnp.broadcast_to(piece[132 + t : 133 + t, :], (16, 128)).astype(jnp.bfloat16))
+    numbers = lax.broadcasted_iota(jnp.int32, (KEYS, 128), 0).astype(jnp.float32).astype(jnp.bfloat16)
+    one, none = jnp.ones((KEYS, 128), jnp.bfloat16), jnp.zeros((KEYS, 128), jnp.bfloat16)
+    for q in range(8):
+        key_row = jnp.broadcast_to(keys[q : q + 1, :], (16, 128)).astype(jnp.bfloat16)
+        key_hot = jnp.where(jnp.concatenate([key_row] * 4, axis=0) == numbers, one, none)
+        code = jnp.broadcast_to(codes[q : q + 1, :], (16, 128)).astype(jnp.bfloat16)
+        lanes = pl.ds(q % 2 * 128, 128)
+        for t in range(16):
+            same = jnp.where(code == tiles[t], one[:16], none[:16])
+            hot[q // 2, t * KEYS : (t + 1) * KEYS, lanes] = key_hot * jnp.concatenate([same] * 4, axis=0)
+
+
+def multiply(c, table, hot, joined_ref, place_ref):
+    places = []
+    for q2 in range(4):
+        out = jnp.dot(table[...], hot[q2], preferred_element_type=jnp.float32)
+        sums = out[:128] + out[128:256]
+        joined_ref[c, q2 * 2] = sums[:, :128].T
+        joined_ref[c, q2 * 2 + 1] = sums[:, 128:].T
+        side = out[256:264] + out[264:272]
+        for h in range(2):
+            places.append(side[0:1, h * 128 : (h + 1) * 128])
+    place_ref[c] = jnp.concatenate(places, axis=0)
 
 
 def gather_kernel(
-    key_hbm, part_hbm, payload_hbm, probe_key_hbm, probe_part_hbm, g_ref, stat_ref,
-    key_ref, part_ref, payload_ref, probe_key, probe_part, sums, parcels,
+    key_hbm, part_hbm, payload_hbm, probe_key_hbm, probe_part_hbm, joined_ref, place_ref, stat_ref,
+    g_ref, table_a, hot_a, table_b, hot_b, key_ref, part_ref, payload_ref, probe_key, probe_part, sums, parcels,
     loads, recv, pair_recv, send, stat_send, stat_recv,
 ):
     yh, z, yl, x, core = (lax.axis_index(a) for a in ALL)
@@ -257,45 +308,75 @@
         landed = g_ref.at[pl.ds(0, 64), rows]
         pltpu.make_async_copy(landed, landed, pair_recv.at[p]).wait()
 
-    now = jnp.concatenate([match_rows(probe_key, probe_part, g_ref), live], axis=0)
-    first = 0
-    for phase in range(4):
-        sums[phase] = now
-        sent = []
+    def parcels_of(phase):
+        copies = []
         for n in range(1 if phase == 0 else 3):
             target = device(here, 1 - core) if phase == 0 else device(shifted(here, phase - 1, n + 1), core)
-            sent.append(
+            at = 3 * phase - 2 + n if phase else 0
+            copies.append(
                 pltpu.make_async_remote_copy(
-                    src_ref=sums.at[phase], dst_ref=parcels.at[first + n], send_sem=stat_send.at[first + n],
-                    recv_sem=stat_recv.at[first + n], device_id=target, device_id_type=MESH,
+                    src_ref=sums.at[phase], dst_ref=parcels.at[at], send_sem=stat_send.at[at],
+                    recv_sem=stat_recv.at[at], device_id=target, device_id_type=MESH,
                 )
             )
-            sent[-1].start()
-        for n, copy in enumerate(sent):
+        return copies
+
+    def begin(phase):
+        for copy in parcels_of(phase):
+            copy.start()
+
+    def finish(phase):
+        now = sums[phase]
+        for n, copy in enumerate(parcels_of(phase)):
             copy.wait_recv()
-            now = now + parcels[first + n]
-        for copy in sent:
+            now = now + parcels[3 * phase - 2 + n if phase else 0]
+        for copy in parcels_of(phase):
             copy.wait_send()
-        first += len(sent)
-    stat_ref[...] = now
+        return now
+
+    sums[0] = jnp.concatenate([match_rows(probe_key, probe_part, g_ref), live], axis=0)
+    begin(0)
+    prepare(0, probe_key, probe_part, g_ref, table_a, hot_a)
+
+    def joins(i, carry):
+        for phase in range(1, 4):
+            @pl.when(i == 2 * phase)
+            def _():
+                sums[phase] = finish(phase - 1)
+                begin(phase)
+
+        prepare(2 * i + 1, probe_key, probe_part, g_ref, table_b, hot_b)
+        multiply(2 * i, table_a, hot_a, joined_ref, place_ref)
+        prepare(jnp.minimum(2 * i + 2, 15), probe_key, probe_part, g_ref, table_a, hot_a)
+        multiply(2 * i + 1, table_b, hot_b, joined_ref, place_ref)
+        return carry
+
+    lax.fori_loop(0, 8, joins, 0)
+    stat_ref[...] = finish(3)
     for p in range(3):
         rows = pl.ds(CUTS[p][0], CUTS[p][1])
         sent = g_ref.at[pl.ds(0, 127), rows]
         pltpu.make_async_copy(sent, sent, send.at[p]).wait()
 
 
-def gather_tables(build_key, build_part, build_payload, probe_key, probe_part):
+def gather_and_join(build_key, build_part, build_payload, probe_key, probe_part):
     hbm = pl.BlockSpec(memory_space=pltpu.HBM)
     vmem = pl.BlockSpec(memory_space=pltpu.VMEM)
     return pl.pallas_call(
         gather_kernel,
         out_shape=(
-            jax.ShapeDtypeStruct((128, PIECE, 128), jnp.float32),
+            jax.ShapeDtypeStruct((16, 8, 128, 128), jnp.float32),
+            jax.ShapeDtypeStruct((16, 8, 128), jnp.float32),
             jax.ShapeDtypeStruct((16, 128), jnp.float32),
         ),
         in_specs=[hbm] * 5,
-        out_specs=(vmem, vmem),
+        out_specs=(vmem, vmem, vmem),
         scratch_shapes=[
+            pltpu.VMEM((128, PIECE, 128), jnp.float32),
+            pltpu.VMEM((272, 1024), jnp.bfloat16),
+            pltpu.VMEM((4, 1024, 256), jnp.bfloat16),
+            pltpu.VMEM((272, 1024), jnp.bfloat16),
+            pltpu.VMEM((4, 1024, 256), jnp.bfloat16),
             pltpu.VMEM((1, 2, 128), jnp.int32),
             pltpu.SMEM((1, 2), jnp.int32),
             pltpu.VMEM((1, 2, 128, 128), jnp.float32),
@@ -311,79 +392,20 @@
             pltpu.SemaphoreType.DMA((10,)),
         ],
         compiler_params=pltpu.CompilerParams(
-            collective_id=0, has_side_effects=True, vmem_limit_bytes=16 * 1024 * 1024
+            collective_id=0, has_side_effects=True, vmem_limit_bytes=40 * 1024 * 1024
         ),
-        name="gather_tables",
-    )(build_key, build_part, build_payload, probe_key, probe_part)
-
-
-def join_kernel(key_ref, part_ref, g_ref, joined_ref, place_ref, table, hot):
-    keys = key_ref[0].astype(jnp.float32)
-    codes = coded(part_ref[0])
-    tiles = []
-    for r in range(8):
-        piece = g_ref[r]
-        high = piece.astype(jnp.bfloat16)
-        low = (piece - high.astype(jnp.float32)).astype(jnp.bfloat16)
-        lanes = pl.ds(r * 128, 128)
-        table[0:128, lanes] = high[:128]
-        table[128:256, lanes] = low[:128]
-        table[256:272, lanes] = jnp.concatenate(
-            [high[128:].astype(jnp.float32), low[128:].astype(jnp.float32)], axis=0
-        ).astype(jnp.bfloat16)
-        for t in range(2):
-            tiles.append(jnp.broadcast_to(piece[132 + t : 133 + t, :], (16, 128)).astype(jnp.bfloat16))
-    numbers = lax.broadcasted_iota(jnp.int32, (KEYS, 128), 0).astype(jnp.float32).astype(jnp.bfloat16)
-    one, none = jnp.ones((KEYS, 128), jnp.bfloat16), jnp.zeros((KEYS, 128), jnp.bfloat16)
-    for q2 in range(4):
-        for h in range(2):
-            q = q2 * 2 + h
-            key_row = jnp.broadcast_to(keys[q : q + 1, :], (16, 128)).astype(jnp.bfloat16)
-            key_hot = jnp.where(jnp.concatenate([key_row] * 4, axis=0) == numbers, one, none)
-            code = jnp.broadcast_to(codes[q : q + 1, :], (16, 128)).astype(jnp.bfloat16)
-            lanes = pl.ds(h * 128, 128)
-            for t in range(16):
-                same = jnp.where(code == tiles[t], one[:16], none[:16])
-                hot[q2, t * KEYS : (t + 1) * KEYS, lanes] = key_hot * jnp.concatenate([same] * 4, axis=0)
-        out = jnp.dot(table[...], hot[q2], preferred_element_type=jnp.float32)
-        sums = out[:128] + out[128:256]
-        joined_ref[0, q2 * 2] = sums[:, :128].T
-        joined_ref[0, q2 * 2 + 1] = sums[:, 128:].T
-        side = out[256:264] + out[264:272]
-        for h in range(2):
-            place_ref[0, q2 * 2 + h : q2 * 2 + h + 1, :] = side[0:1, h * 128 : (h + 1) * 128]
-
-
-def join(probe_key, probe_part, tables):
-    return pl.pallas_call(
-        join_kernel,
-        grid=(16,),
-        out_shape=(
-            jax.ShapeDtypeStruct((16, 8, 128, 128), jnp.float32),
-            jax.ShapeDtypeStruct((16, 8, 128), jnp.float32),
-        ),
-        in_specs=[
-            pl.BlockSpec((1, 8, 128), lambda c: (c, 0, 0)),
-            pl.BlockSpec((1, 8, 128), lambda c: (c, 0, 0)),
-            pl.BlockSpec((8, PIECE, 128), lambda c: (c, 0, 0)),
-        ],
-        out_specs=(
-            pl.BlockSpec((1, 8, 128, 128), lambda c: (c, 0, 0, 0)),
-            pl.BlockSpec((1, 8, 128), lambda c: (c, 0, 0)),
-        ),
-        scratch_shapes=[
-            pltpu.VMEM((272, 1024), jnp.bfloat16),
-            pltpu.VMEM((4, 1024, 256), jnp.bfloat16),
-        ],
-        compiler_params=pltpu.CompilerParams(vmem_limit_bytes=32 * 1024 * 1024),
-        name="join",
-    )(probe_key, probe_part, tables)
+        name="gather_and_join",
+    )(
+        *(
+            pltpu.with_memory_space_constraint(a, pltpu.HBM)
+            for a in (build_key, build_part, build_payload, probe_key, probe_part)
+        )
+    )
 
 
 def local(build_key, build_part, build_payload, probe_key, probe_part):
     probe_key, probe_part = probe_key.reshape(16, 8, 128), probe_part.reshape(16, 8, 128)
-    tables, stats = gather_tables(build_key, build_part, build_payload, probe_key, probe_part)
-    joined, places = join(probe_key, probe_part, tables)
+    joined, places, stats = gather_and_join(build_key, build_part, build_payload, probe_key, probe_part)
     rate = stats[:8].reshape(PARTS_SIZE) / jnp.maximum(stats[8:].reshape(PARTS_SIZE), 1.0)
     return (joined[None, None], places[None, None], rate)
 

time: 70.6 us -> 54.1 us (0.77)
  the two profiles are of different devices: /device:TPU:0 before, /device:TPU:1 now
where the time goes in v3:
time: 54.1 us; the launch traced here: 54 us
  Pallas kernels  48.7 us (90%)
  local copies, waits for them, and re-layouts  4.03 us (7%)
  between operations  0.64 us (1%)
  other arithmetic  0.6 us (1%)
    pallas_call x1, Pallas kernels, gather_and_join(): pl.pallas_call(gather_kernel, out_shape=(jax.ShapeDtypeStruct((16, 8, 128...  48.7 us
    unnamed x2, local copies, waits for them, and re-layouts  4.03 us

profile of v3, /device:TPU:1, one launch (start us, length us, event | category | flops | bytes accessed | tf_op | source)
XLA Modules:
  0.0 54.0 jit_solution(2657527019201769295)
XLA Ops:
  0.6 48.7 %gather_and_join.1 = (f32[16,8,128,128]{3,2,1,0:T(8,128)S(1)}, f32[16,8,128]{2,1,0:T(8,128)S(1)}, f32[16,128]{1,0:T(8,128)S(1)}) custom-call(s32[1,2,128]{2,1,0:T(2,128)} %key_hbm.1, s32[1,2]{1,0:T(1,128)} %part_hbm.1, f32[1,2,128,128]{3,2,1,0:T(8,128)} %payload_hbm.1, s32[16,8,128]{2,1,0:T(8,128)} %bitcast.8, s32[16,8,128]{2,1,0:T(8,128)} %bitcast.9), custom_call_target="tpu_custom_call" | custom-call | tf_op jit(solution)/shard_map/gather_and_join/pallas_call | solution.py:365
  49.4 0.6 %divide_bitcast_fusion = f32[1024]{0:T(1024)} fusion(f32[16,128]{1,0:T(8,128)S(1)} %get-tuple-element.8), kind=kLoop, calls=%fused_computation | loop fusion | flops 2048 | bytes 12288 | tf_op jit(solution)/shard_map/div | solution.py:409
  50.0 3.4 %copy.10 = f32[1,1,16,8,128,128]{5,4,3,2,1,0:T(8,128)} copy(f32[1,1,16,8,128,128]{5,4,3,2,1,0:T(8,128)S(1)} %bitcast.6) | data formatting | bytes 16777216
  53.4 0.6 %copy.11 = f32[1,1,16,8,128]{4,3,2,1,0:T(8,128)} copy(f32[1,1,16,8,128]{4,3,2,1,0:T(8,128)S(1)} %bitcast.7) | data formatting | bytes 131072

commit v4 on v3

--- a/solution.py
+++ b/solution.py
@@ -10,6 +10,7 @@
 
 PARTS_SIZE = 1024
 KEYS = 64
+EARLY = 14
 ROW = ("row_0", "row_1")
 COL = ("col_0", "col_1", "col_2")
 ALL = ROW + COL
@@ -111,12 +112,13 @@
     return lax.fori_loop(0, 4, columns, jnp.zeros((8, 128), jnp.float32))
 
 
-def prepare(c, key_ref, part_ref, g_ref, table, hot):
+def prepare(c, key_ref, part_ref, g_ref, table, hot, column=None):
+    column = c if column is None else column
     keys = key_ref[c].astype(jnp.float32)
     codes = coded(part_ref[c])
     tiles = []
     for r in range(8):
-        piece = g_ref[c * 8 + r]
+        piece = g_ref[column * 8 + r]
         high = piece.astype(jnp.bfloat16)
         low = (piece - high.astype(jnp.float32)).astype(jnp.bfloat16)
         lanes = pl.ds(r * 128, 128)
@@ -153,8 +155,8 @@
 
 
 def gather_kernel(
-    key_hbm, part_hbm, payload_hbm, probe_key_hbm, probe_part_hbm, joined_ref, place_ref, stat_ref,
-    g_ref, table_a, hot_a, table_b, hot_b, key_ref, part_ref, payload_ref, probe_key, probe_part, sums, parcels,
+    key_hbm, part_hbm, payload_hbm, probe_key_hbm, probe_part_hbm, joined_ref, place_ref, stat_ref, g_ref,
+    table_a, hot_a, table_b, hot_b, key_ref, part_ref, payload_ref, probe_key, probe_part, sums, parcels,
     loads, recv, pair_recv, send, stat_send, stat_recv,
 ):
     yh, z, yl, x, core = (lax.axis_index(a) for a in ALL)
@@ -214,7 +216,7 @@
 
     barrier = pltpu.get_barrier_semaphore()
     for dim in range(3):
-        for delta in (1, 3):
+        for delta in (1, 2, 3):
             pl.semaphore_signal(barrier, inc=1, device_id=device(shifted(here, dim, delta), core), device_id_type=MESH)
     pl.semaphore_signal(barrier, inc=1, device_id=device(here, 1 - core), device_id_type=MESH)
 
@@ -224,34 +226,25 @@
     own = slot(here, core)
     g_ref[own, :128, :] = table
     g_ref[own, 128:, :] = side
-    pl.semaphore_wait(barrier, 7)
-
-    def both(p, off, level):
-        push(p, off, level, 1)
-        push(p, off, level, -1)
+    pl.semaphore_wait(barrier, 10)
+
+    def spread(p, off, level):
+        for delta in (2, 1, -1) if level < 2 else (1, -1):
+            push(p, off, level, delta)
 
     for level in range(3):
         for p in range(3):
-            both(p, (0, 0, 0), level)
+            spread(p, (0, 0, 0), level)
     for p in range(3):
         pair(p, (0, 0, 0))
     for copy in incoming[3:]:
         copy.wait()
     live = live_rows(probe_key, probe_part)
-    for p in range(3):
-        arrive(p, (3, 0, 0))
-        push(p, (3, 0, 0), 0, 1)
-    for level in (1, 2):
-        for p in range(3):
-            both(p, (3, 0, 0), level)
-    for p in range(3):
-        arrive(p, (1, 0, 0))
-        both(p, (1, 0, 0), 1)
-        both(p, (1, 0, 0), 2)
-    for p in range(3):
-        arrive(p, (2, 0, 0))
-        both(p, (2, 0, 0), 1)
-        both(p, (2, 0, 0), 2)
+    for o in (3, 1, 2):
+        for p in range(3):
+            arrive(p, (o, 0, 0))
+            spread(p, (o, 0, 0), 1)
+            spread(p, (o, 0, 0), 2)
     for p in range(3):
         for o in (3, 1, 2):
             pair(p, (o, 0, 0))
@@ -261,14 +254,10 @@
 
     def second(i, carry):
         da = turn(i)
-        delta = 1 - 2 * (da % 2)
-        for p in range(3):
-            near = (4 - delta) % 4
+        for p in range(3):
             for o in (3, 1):
                 arrive(p, (da, o, 0))
-                both(p, (da, o, 0), 2)
-            push(p, (da, near, 0), 1, delta)
-            for o in (3, 1):
+                spread(p, (da, o, 0), 2)
                 pair(p, (da, o, 0))
         return carry
 
@@ -276,7 +265,7 @@
         da = turn(i)
         for p in range(3):
             arrive(p, (da, 2, 0))
-            both(p, (da, 2, 0), 2)
+            spread(p, (da, 2, 0), 2)
             pair(p, (da, 2, 0))
         return carry
 
@@ -340,18 +329,18 @@
 
     def joins(i, carry):
         for phase in range(1, 4):
-            @pl.when(i == 2 * phase)
+            @pl.when(i == 2 * phase - (phase == 1))
             def _():
                 sums[phase] = finish(phase - 1)
                 begin(phase)
 
         prepare(2 * i + 1, probe_key, probe_part, g_ref, table_b, hot_b)
         multiply(2 * i, table_a, hot_a, joined_ref, place_ref)
-        prepare(jnp.minimum(2 * i + 2, 15), probe_key, probe_part, g_ref, table_a, hot_a)
+        prepare(jnp.minimum(2 * i + 2, EARLY - 1), probe_key, probe_part, g_ref, table_a, hot_a)
         multiply(2 * i + 1, table_b, hot_b, joined_ref, place_ref)
         return carry
 
-    lax.fori_loop(0, 8, joins, 0)
+    lax.fori_loop(0, EARLY // 2, joins, 0)
     stat_ref[...] = finish(3)
     for p in range(3):
         rows = pl.ds(CUTS[p][0], CUTS[p][1])
@@ -365,14 +354,14 @@
     return pl.pallas_call(
         gather_kernel,
         out_shape=(
-            jax.ShapeDtypeStruct((16, 8, 128, 128), jnp.float32),
-            jax.ShapeDtypeStruct((16, 8, 128), jnp.float32),
+            jax.ShapeDtypeStruct((EARLY, 8, 128, 128), jnp.float32),
+            jax.ShapeDtypeStruct((EARLY, 8, 128), jnp.float32),
             jax.ShapeDtypeStruct((16, 128), jnp.float32),
+            jax.ShapeDtypeStruct((128, PIECE, 128), jnp.float32),
         ),
         in_specs=[hbm] * 5,
-        out_specs=(vmem, vmem, vmem),
+        out_specs=(vmem, vmem, vmem, vmem),
         scratch_shapes=[
-            pltpu.VMEM((128, PIECE, 128), jnp.float32),
             pltpu.VMEM((272, 1024), jnp.bfloat16),
             pltpu.VMEM((4, 1024, 256), jnp.bfloat16),
             pltpu.VMEM((272, 1024), jnp.bfloat16),
@@ -392,7 +381,7 @@
             pltpu.SemaphoreType.DMA((10,)),
         ],
         compiler_params=pltpu.CompilerParams(
-            collective_id=0, has_side_effects=True, vmem_limit_bytes=40 * 1024 * 1024
+            collective_id=0, has_side_effects=True, vmem_limit_bytes=20 * 1024 * 1024
         ),
         name="gather_and_join",
     )(
@@ -403,11 +392,85 @@
     )
 
 
+def finish_kernel(
+    key_hbm, part_hbm, early_ref, early_place_ref, stat_ref, g_ref, joined_hbm, place_hbm, rate_hbm,
+    probe_key, probe_part, joined_ref, place_ref, rate_ref, table_a, hot_a, table_b, hot_b, loads, stores,
+):
+    late = 16 - EARLY
+    incoming = [
+        pltpu.make_async_copy(src.at[pl.ds(EARLY, late)], dst, loads.at[n])
+        for n, (src, dst) in enumerate(((key_hbm, probe_key), (part_hbm, probe_part)))
+    ]
+    for copy in incoming:
+        copy.start()
+    outgoing = [
+        pltpu.make_async_copy(early_ref, joined_hbm.at[pl.ds(0, EARLY)], stores.at[0]),
+        pltpu.make_async_copy(early_place_ref, place_hbm.at[pl.ds(0, EARLY)], stores.at[1]),
+    ]
+    for copy in outgoing:
+        copy.start()
+    rate_ref[...] = stat_ref[0:8, :] / jnp.maximum(stat_ref[8:16, :], 1.0)
+    outgoing.append(pltpu.make_async_copy(rate_ref, rate_hbm, stores.at[2]))
+    outgoing[-1].start()
+    for copy in incoming:
+        copy.wait()
+    buffers = ((table_a, hot_a), (table_b, hot_b))
+
+    def ready(n):
+        prepare(n, probe_key, probe_part, g_ref, *buffers[n % 2], EARLY + n)
+
+    ready(0)
+    for n in range(late):
+        if n + 1 < late:
+            ready(n + 1)
+        multiply(n, *buffers[n % 2], joined_ref, place_ref)
+        outgoing.append(pltpu.make_async_copy(joined_ref.at[n], joined_hbm.at[EARLY + n], stores.at[3 + n]))
+        outgoing[-1].start()
+    outgoing.append(pltpu.make_async_copy(place_ref, place_hbm.at[pl.ds(EARLY, late)], stores.at[3 + late]))
+    outgoing[-1].start()
+    for copy in outgoing:
+        copy.wait()
+
+
+def finish_join(probe_key, probe_part, early, early_places, stats, tables):
+    hbm = pl.BlockSpec(memory_space=pltpu.HBM)
+    vmem = pl.BlockSpec(memory_space=pltpu.VMEM)
+    late = 16 - EARLY
+    return pl.pallas_call(
+        finish_kernel,
+        out_shape=(
+            jax.ShapeDtypeStruct((16, 8, 128, 128), jnp.float32),
+            jax.ShapeDtypeStruct((16, 8, 128), jnp.float32),
+            jax.ShapeDtypeStruct((8, 128), jnp.float32),
+        ),
+        in_specs=[hbm, hbm, vmem, vmem, vmem, vmem],
+        out_specs=(hbm, hbm, hbm),
+        scratch_shapes=[
+            pltpu.VMEM((late, 8, 128), jnp.int32),
+            pltpu.VMEM((late, 8, 128), jnp.int32),
+            pltpu.VMEM((late, 8, 128, 128), jnp.float32),
+            pltpu.VMEM((late, 8, 128), jnp.float32),
+            pltpu.VMEM((8, 128), jnp.float32),
+            pltpu.VMEM((272, 1024), jnp.bfloat16),
+            pltpu.VMEM((4, 1024, 256), jnp.bfloat16),
+            pltpu.VMEM((272, 1024), jnp.bfloat16),
+            pltpu.VMEM((4, 1024, 256), jnp.bfloat16),
+            pltpu.SemaphoreType.DMA((2,)),
+            pltpu.SemaphoreType.DMA((4 + late,)),
+        ],
+        compiler_params=pltpu.CompilerParams(vmem_limit_bytes=24 * 1024 * 1024),
+        name="finish_join",
+    )(
+        *(pltpu.with_memory_space_constraint(a, pltpu.HBM) for a in (probe_key, probe_part)),
+        early, early_places, stats, tables,
+    )
+
+
 def local(build_key, build_part, build_payload, probe_key, probe_part):
     probe_key, probe_part = probe_key.reshape(16, 8, 128), probe_part.reshape(16, 8, 128)
-    joined, places, stats = gather_and_join(build_key, build_part, build_payload, probe_key, probe_part)
-    rate = stats[:8].reshape(PARTS_SIZE) / jnp.maximum(stats[8:].reshape(PARTS_SIZE), 1.0)
-    return (joined[None, None], places[None, None], rate)
+    early, early_places, stats, tables = gather_and_join(build_key, build_part, build_payload, probe_key, probe_part)
+    joined, places, rate = finish_join(probe_key, probe_part, early, early_places, stats, tables)
+    return (joined[None, None], places[None, None], rate.reshape(PARTS_SIZE))
 
 
 def solution(mesh):

time: 54.1 us -> 50.9 us (0.941)
  local copies, waits for them, and re-layouts: 4.03 us -> 0 us
  Pallas kernels: 48.7 us -> 50.1 us
  other arithmetic: 0.6 us -> 0 us
    unnamed x2 -> x0, local copies, waits for them, and re-layouts: 4.03 us -> none
    pallas_call x1 -> x2, Pallas kernels: 48.7 us -> 50.1 us  [the longest x1 46.6 us: gather_and_join(): pl.pallas_call(gather_kernel, out_shape=(jax.ShapeDtypeStruct((EARLY, 8,...]
    div x1 -> x0, other arithmetic: 0.6 us -> none  [local(): stats[:8].reshape(PARTS_SIZE)]
where the time goes in v4:
time: 50.9 us; the launch traced here: 50.7 us
  Pallas kernels  50.1 us (98%)
  between operations  0.64 us (1%)
    pallas_call x1, Pallas kernels, gather_and_join(): pl.pallas_call(gather_kernel, out_shape=(jax.ShapeDtypeStruct((EARLY, 8,...  46.6 us
    pallas_call x1, Pallas kernels, finish_join(): pl.pallas_call(finish_kernel, out_shape=(jax.ShapeDtypeStruct((16, 8, 128...  3.46 us

profile of v4, /device:TPU:1, one launch (start us, length us, event | category | flops | bytes accessed | tf_op | source)
XLA Modules:
  0.0 50.7 jit_solution(15692207456266334166)
XLA Ops:
  0.6 46.6 %gather_and_join.1 = (f32[14,8,128,128]{3,2,1,0:T(8,128)S(1)}, f32[14,8,128]{2,1,0:T(8,128)S(1)}, f32[16,128]{1,0:T(8,128)S(1)}, f32[128,136,128]{2,1,0:T(8,128)S(1)}) custom-call(s32[1,2,128]{2,1,0:T(2,128)} %key_hbm.1, s32[1,2]{1,0:T(1,128)} %part_hbm.1, f32[1,2,128,128]{3,2,1,0:T(8,128)} %payload_hbm.1, s32[16,8,128]{2,1,0:T(8,128)} %bitcast.5, ...), custom_call_target="tpu_custom_call" | custom-call | tf_op jit(solution)/shard_map/gather_and_join/pallas_call | solution.py:354
  47.2 3.5 %finish_join.1 = (f32[16,8,128,128]{3,2,1,0:T(8,128)}, f32[16,8,128]{2,1,0:T(8,128)}, f32[8,128]{1,0:T(8,128)}) custom-call(s32[16,8,128]{2,1,0:T(8,128)} %bitcast.6, s32[16,8,128]{2,1,0:T(8,128)} %bitcast.8, f32[14,8,128,128]{3,2,1,0:T(8,128)S(1)} %get-tuple-element.10.early_ref, f32[14,8,128]{2,1,0:T(8,128)S(1)} %get-tuple-element.11.early_place_ref, ...), custom_call_target="tpu_custom_call" | custom-call | tf_op jit(solution)/shard_map/finish_join/pallas_call | solution.py:439
